TPU v7x, 32 devices: a whole 2x2x4 slice. The times are simulated.
32 devices in a mesh: ta: 2 (over x), sa: 16 (over z, y, core).
Axes of the slice: x: 2, y: 2, z: 4, core: 2. Of those that a mesh axis runs over, the one named last changes fastest.
Arguments:
- eigvecs: bfloat16 [12, 2, 3, 6912, 128], P('ta', None, None, 'sa'), may hold values from -0.0390625 to 0.0390625
- solutions: bfloat16 [12, 2, 3, 6912, 128], P('ta', None, None, 'sa'), may hold values from -6 to 6
Outputs:
- tau: float32 [12, 2, 128, 128], P('ta', None, 'sa')
- corr: float32 [12], replicated
All inputs are finite; a program needn't handle non-finite values.
Results may differ from a plain program's by a relative error of at most 0.0003.
Values sent between devices are 32-bit elements; how exact they have to be, the bound alone decides.
A program may use at most 64 MiB of HBM per device.

v0:
```python
import jax
import jax.numpy as jnp
from jax import lax
from jax.sharding import PartitionSpec as P


def per_device(eigvecs, solutions):
    slices = eigvecs.shape[0]
    vec_re = eigvecs[:, 0].reshape(slices, -1, eigvecs.shape[-1])
    vec_im = eigvecs[:, 1].reshape(slices, -1, eigvecs.shape[-1])
    sol_re = solutions[:, 0].reshape(slices, -1, solutions.shape[-1])
    sol_im = solutions[:, 1].reshape(slices, -1, solutions.shape[-1])

    def contract(left, right):
        return jnp.einsum("tka,tkb->tab", left, right, preferred_element_type=jnp.float32)

    real_part = contract(vec_re, sol_re) + contract(vec_im, sol_im)
    imag_part = contract(vec_re, sol_im) - contract(vec_im, sol_re)
    partial_tau = jnp.stack([real_part, imag_part], 1)
    scale = 1.0 / (2.0 * partial_tau.shape[2] * partial_tau.shape[3])
    tau = lax.psum_scatter(partial_tau, "sa", scatter_dimension=2, tiled=True)
    row_norms = jnp.sum(tau * tau, axis=(1, 2, 3))
    corr_local = lax.psum(row_norms, "sa") * scale
    corr = lax.all_gather(corr_local, "ta", axis=0, tiled=True)
    return (tau, corr)


def solution(mesh):
    in_specs = (P("ta", None, None, "sa", None), P("ta", None, None, "sa", None))
    out_specs = (P("ta", None, "sa", None), P())
    return jax.shard_map(
        per_device, mesh=mesh, in_specs=in_specs, out_specs=out_specs, check_vma=False
    )
```

profile of v0, /device:TPU:0, one launch (start us, length us, event | category | flops | bytes accessed | tf_op | source)
XLA Modules:
  0.0 119.6 jit_solution(2709096211975738395)
XLA Ops:
  7.2 0.0 reduce-scatter.2.cloned.1.call-start
  7.2 0.0 copy-start
  7.2 2.6 %fusion.3 = (bf16[6,1,3,432,128]{4,3,2,1,0:T(8,128)(2,1)S(1)}, bf16[6,1,3,432,128]{4,3,2,1,0:T(8,128)(2,1)S(1)}) fusion(bf16[6,2,3,432,128]{4,3,2,1,0:T(8,128)(2,1)} %param.2), kind=kLoop, calls=%fused_computation.8 | loop fusion | bytes 7962624 | tf_op jit(solution)/shard_map/slice | solution.py:10
  9.8 0.7 copy-done
  10.5 0.3 fusion.2
  10.8 0.8 fusion.4
  11.6 0.9 fusion.5
  12.5 0.8 fusion.1
  13.3 0.9 fusion
  14.2 0.0 copy-start.1
  14.2 0.9 pad_maximum_fusion
  15.2 0.0 reduce-scatter.2.cloned.1.call-update
  15.2 0.0 copy-done.1
  15.2 0.6 dynamic-slice
  15.8 59.0 %reduce-scatter.2.cloned.1.call-done = f32[6,2,8,128]{3,2,0,1:T(8,128)} async-done(((f32[6,2,128,128]{3,2,0,1:T(8,128)}), f32[6,2,8,128]{3,2,0,1:T(8,128)}) %reduce-scatter.2.cloned.1.call-update) | async-done | bytes 49168 | tf_op jit(solution)/shard_map/reduce_scatter | solution.py:21
  74.8 0.9 multiply_reduce_fusion
  76.3 29.5 %psum.7 = f32[6]{0:T(128)S(1)} all-reduce(f32[6]{0:T(128)S(1)} %multiply_reduce_fusion), channel_id=1, replica_groups=mesh['ta'=2,'sa'=16] {'sa'}, use_global_device_ids=true, to_apply=%region_2.0 | all-reduce | flops 6 | bytes 48 | tf_op jit(solution)/shard_map/psum | solution.py:23
  105.8 0.1 multiply_dynamic-update-slice_fusion
  105.9 5.4 %all-reduce = f32[12]{0:T(128)} all-reduce(f32[12]{0:T(128)S(1)} %multiply_dynamic-update-slice_fusion), channel_id=1, replica_groups=mesh['ta'=2,'sa'=16] {'ta'}, use_global_device_ids=true, to_apply=%add | all-reduce | flops 12 | bytes 96
  111.3 1.4 %copy.4 = f32[6,2,8,128]{3,2,1,0:T(8,128)} copy(f32[6,2,8,128]{3,2,0,1:T(8,128)} %reduce-scatter.2.cloned.1.call-done) | data formatting | bytes 98304
  (1 shorter events, 0.0 us)
Async XLA Ops:
  7.2 67.6 %reduce-scatter.2.cloned.1.call-start = ((), (), s32[]{:S(2)}) async-start(), calls=%async_computation.1 | async-start | bytes 835584 | tf_op jit(solution)/shard_map/reduce_scatter | solution.py:21
  7.2 3.3 %copy-start = (bf16[6,2,3,432,128]{4,3,2,1,0:T(8,128)(2,1)S(1)}, bf16[6,2,3,432,128]{4,3,2,1,0:T(8,128)(2,1)}, u32[]{:S(2)}) copy-start(bf16[6,2,3,432,128]{4,3,2,1,0:T(8,128)(2,1)} %param.3) | copy-start | bytes 11943940
  14.2 1.0 copy-start.1
Sparse Core Ops, SparseCore 0:
  15.3 59.4 reduce-scatter.1
where the time goes:
time: 120 us
  waiting for transfers between devices  59 us (49%)
  blocking collectives  34.9 us (29%)
  between operations  14.7 us (12%)
  local copies, waits for them, and re-layouts  5.59 us (5%)
  matrix products  3.39 us (3%)
  other arithmetic  1.95 us (2%)
    reduce_scatter x1, waiting for transfers between devices, per_device(): tau = lax.psum_scatter(partial_tau, 'sa', scatter_dimension=2, tiled=True)  59 us
    psum x1, blocking collectives, per_device(): corr_local = lax.psum(row_norms, 'sa') * scale  29.5 us
    unnamed x1, blocking collectives  5.41 us
    dot_general x4, matrix products, contract(): jnp.einsum('tka,tkb->tab', left, right, preferred_element_type=jnp.float32)  3.39 us
    unnamed x7, local copies, waits for them, and re-layouts  2.76 us
    slice x1, local copies, waits for them, and re-layouts, per_device(): vec_im = eigvecs[:, 1].reshape(slices, -1, eigvecs.shape[-1])  2.57 us
  transfers between devices with their start and end apart: 1, of which 1 were waited for; matrix products, arithmetic and copies ran while one was open for 0% of the time, Pallas kernels for 0%

commit v1 on v0

v1 whole, which is shorter than its diff:
```python
import functools

import jax
import jax.numpy as jnp
from jax import lax
from jax.experimental import pallas as pl
from jax.experimental.pallas import tpu as pltpu
from jax.sharding import PartitionSpec as P

LANES = 128


def split_of(n):
    cores = 2 if n % 2 == 0 else 1
    rest = n // cores
    ys = 1
    while rest % (ys * 2) == 0 and (ys * 2) * (ys * 2) <= rest:
        ys *= 2
    return rest // ys, ys, cores


def kernel(dims, vec_hbm, sol_hbm, tau_ref, corr_ref,
           vec, sol, part, got_core, half, got_y, quarter, got_z, norms,
           load_sem, core_send, core_recv, y_send, y_recv, z_send, z_recv, n_send, n_recv):
    n_ta, n_sa, zs, ys, cores = dims
    slices = vec_hbm.shape[0]
    rows = tau_ref.shape[2]
    ta, me = lax.axis_index("ta"), lax.axis_index("sa")
    core = lax.rem(me, cores)
    my_y = lax.rem(me // cores, ys)
    my_z = me // (cores * ys)

    def core_peer(j):
        return me - core + lax.rem(core + j, cores)

    def y_peer(j):
        return lax.rem(my_y + j, ys)

    def z_peer(j):
        return lax.rem(my_z + j, zs)

    def at(z, y, c):
        return (z * ys + y) * cores + c

    loads = []
    for t in range(slices):
        pair = (pltpu.make_async_copy(vec_hbm.at[t], vec.at[t], load_sem.at[t, 0]),
                pltpu.make_async_copy(sol_hbm.at[t], sol.at[t], load_sem.at[t, 1]))
        for one in pair:
            one.start()
        loads.append(pair)

    barrier = pltpu.get_barrier_semaphore()
    greeted = 0
    for j in range(1, cores):
        pl.semaphore_signal(barrier, inc=1, device_id={"ta": ta, "sa": core_peer(j)})
        greeted += 1
    for j in range(1, ys):
        pl.semaphore_signal(barrier, inc=1, device_id={"ta": ta, "sa": at(my_z, y_peer(j), core)})
        greeted += 1
    for j in range(1, zs):
        pl.semaphore_signal(barrier, inc=1, device_id={"ta": ta, "sa": at(z_peer(j), my_y, core)})
        greeted += 1
    for j in range(1, n_ta):
        pl.semaphore_signal(barrier, inc=1, device_id={"ta": lax.rem(ta + j, n_ta), "sa": me})
        greeted += 1

    def core_copies(t):
        return [pltpu.make_async_remote_copy(
            src_ref=part.at[t, lax.rem(core + j, cores)], dst_ref=got_core.at[t, j - 1],
            send_sem=core_send.at[t, j - 1], recv_sem=core_recv.at[t, j - 1],
            device_id={"ta": ta, "sa": core_peer(j)}) for j in range(1, cores)]

    def y_copies(t):
        return [pltpu.make_async_remote_copy(
            src_ref=half.at[t, y_peer(j)], dst_ref=got_y.at[t, j - 1],
            send_sem=y_send.at[t, j - 1], recv_sem=y_recv.at[t, j - 1],
            device_id={"ta": ta, "sa": at(my_z, y_peer(j), core)}) for j in range(1, ys)]

    def z_copies(t):
        return [pltpu.make_async_remote_copy(
            src_ref=quarter.at[t, z_peer(j)], dst_ref=got_z.at[t, j - 1],
            send_sem=z_send.at[t, j - 1], recv_sem=z_recv.at[t, j - 1],
            device_id={"ta": ta, "sa": at(z_peer(j), my_y, core)}) for j in range(1, zs)]

    def compute(t):
        for one in loads[t]:
            one.wait()
        flat = (-1, vec.shape[-1])
        left = jnp.concatenate([vec[t, 0].reshape(flat), vec[t, 1].reshape(flat)], axis=1)
        right = jnp.concatenate([sol[t, 0].reshape(flat), sol[t, 1].reshape(flat)], axis=1)
        full = lax.dot_general(left, right, (((0,), (0,)), ((), ())), preferred_element_type=jnp.float32)
        nev, nb = vec.shape[-1], sol.shape[-1]
        both = (full[:nev, :nb] + full[nev:, nb:], full[:nev, nb:] - full[nev:, :nb])
        for p in range(2):
            for d in range(n_sa):
                c, y, z = d % cores, d // cores % ys, d // (cores * ys)
                part[t, c, y, z, p] = both[p][d * rows:(d + 1) * rows]
        if t == 0:
            pl.semaphore_wait(barrier, greeted)
        for one in core_copies(t):
            one.start()

    def after_core(t):
        for one in core_copies(t):
            one.wait_recv()
        total = part[t, core]
        for j in range(1, cores):
            total = total + got_core[t, j - 1]
        half[t] = total
        for one in y_copies(t):
            one.start()

    def after_y(t):
        for one in y_copies(t):
            one.wait_recv()
        total = half[t, my_y]
        for j in range(1, ys):
            total = total + got_y[t, j - 1]
        quarter[t] = total
        for one in z_copies(t):
            one.start()

    def after_z(t):
        for one in z_copies(t):
            one.wait_recv()
        total = quarter[t, my_z]
        for j in range(1, zs):
            total = total + got_z[t, j - 1]
        tau_ref[t] = total
        square = total * total
        return jnp.sum(square[0] + square[1], axis=0, keepdims=True)

    lag = 2
    for t in range(slices + lag):
        if t < slices:
            compute(t)
        if t >= lag:
            after_core(t - lag)
    for t in range(slices):
        after_y(t)
    width = norms.shape[-1]
    lane = lax.broadcasted_iota(jnp.int32, (1, width), 1)
    mine = jnp.zeros((1, width), jnp.float32)
    for t in range(slices):
        norm = jnp.sum(after_z(t), axis=1, keepdims=True)
        mine = mine + jnp.where(lane == ta * slices + t, norm, 0.0)
    place = ta * n_sa + me
    norms[place] = mine
    everyone = n_ta * n_sa

    def norm_copy(j):
        peer = lax.rem(place + j, everyone)
        return pltpu.make_async_remote_copy(
            src_ref=norms.at[place], dst_ref=norms.at[place],
            send_sem=n_send, recv_sem=n_recv,
            device_id={"ta": peer // n_sa, "sa": lax.rem(peer, n_sa)})

    @pl.loop(1, everyone)
    def _(j):
        norm_copy(j).start()

    for t in range(slices):
        for one in core_copies(t) + y_copies(t) + z_copies(t):
            one.wait_send()
    rest = norms.at[pl.ds(0, everyone - 1)]
    whole = pltpu.make_async_remote_copy(
        src_ref=rest, dst_ref=rest, send_sem=n_send, recv_sem=n_recv,
        device_id={"ta": ta, "sa": core_peer(1)})
    whole.wait_recv()
    scale = 1.0 / (2.0 * vec.shape[-1] * sol.shape[-1])
    corr_ref[...] = jnp.sum(norms[...], axis=0) * scale
    whole.wait_send()


def solution(mesh):
    n_ta, n_sa = mesh.shape["ta"], mesh.shape["sa"]
    zs, ys, cores = split_of(n_sa)

    def per_device(vecs, sols):
        slices, nev, nb = vecs.shape[0], vecs.shape[-1], sols.shape[-1]
        rows = nev // n_sa
        width = -(-n_ta * slices // LANES) * LANES
        f32 = jnp.float32
        block = (2, rows, nb)
        dma = pltpu.SemaphoreType.DMA
        tau, corr = pl.pallas_call(
            functools.partial(kernel, (n_ta, n_sa, zs, ys, cores)),
            out_shape=(jax.ShapeDtypeStruct((slices, 2, rows, nb), f32),
                       jax.ShapeDtypeStruct((1, width), f32)),
            in_specs=[pl.BlockSpec(memory_space=pltpu.HBM)] * 2,
            out_specs=[pl.BlockSpec(memory_space=pltpu.VMEM)] * 2,
            scratch_shapes=[
                pltpu.VMEM(vecs.shape, vecs.dtype),
                pltpu.VMEM(sols.shape, sols.dtype),
                pltpu.VMEM((slices, cores, ys, zs) + block, f32),
                pltpu.VMEM((slices, max(cores - 1, 1), ys, zs) + block, f32),
                pltpu.VMEM((slices, ys, zs) + block, f32),
                pltpu.VMEM((slices, max(ys - 1, 1), zs) + block, f32),
                pltpu.VMEM((slices, zs) + block, f32),
                pltpu.VMEM((slices, max(zs - 1, 1)) + block, f32),
                pltpu.VMEM((n_ta * n_sa, 1, width), f32),
                dma((slices, 2)),
                dma((slices, max(cores - 1, 1))), dma((slices, max(cores - 1, 1))),
                dma((slices, max(ys - 1, 1))), dma((slices, max(ys - 1, 1))),
                dma((slices, max(zs - 1, 1))), dma((slices, max(zs - 1, 1))),
                dma, dma,
            ],
            compiler_params=pltpu.CompilerParams(
                collective_id=0, has_side_effects=True, vmem_limit_bytes=48 * 1024 * 1024),
        )(vecs, sols)
        return tau, corr[0, :n_ta * slices]

    in_specs = (P("ta", None, None, "sa", None), P("ta", None, None, "sa", None))
    out_specs = (P("ta", None, "sa", None), P())
    return jax.shard_map(per_device, mesh=mesh, in_specs=in_specs, out_specs=out_specs, check_vma=False)
```

time: 120 us -> 27.4 us (0.23)
  waiting for transfers between devices: 59 us -> 0 us
  blocking collectives: 34.9 us -> 0 us
  Pallas kernels: 0 us -> 23.4 us
  between operations: 14.7 us -> 0.65 us
  matrix products: 3.39 us -> 0 us
  local copies, waits for them, and re-layouts: 5.59 us -> 3.25 us
  other arithmetic: 1.95 us -> 0 us
    reduce_scatter x1 -> x0, waiting for transfers between devices: 59 us -> none  [per_device(): tau = lax.psum_scatter(partial_tau, 'sa', scatter_dimension=2, tiled=True)]
    psum x1 -> x0, blocking collectives: 29.5 us -> none  [per_device(): corr_local = lax.psum(row_norms, 'sa') * scale]
    pallas_call x0 -> x1, Pallas kernels: none -> 23.4 us  [per_device(): pl.pallas_call(functools.partial(kernel, (n_ta, n_sa, zs, ys, cores)), ou...]
    unnamed x1 -> x0, blocking collectives: 5.41 us -> none
    dot_general x4 -> x0, matrix products: 3.39 us -> none  [contract(): jnp.einsum('tka,tkb->tab', left, right, preferred_element_type=jnp.float32)]
    slice x2 -> x0, local copies, waits for them, and re-layouts: 2.82 us -> none  [the longest x1 2.57 us: per_device(): vec_im = eigvecs[:, 1].reshape(slices, -1, eigvecs.shape[-1])]
    unnamed x7 -> x3, local copies, waits for them, and re-layouts: 2.76 us -> 2.74 us
  transfers between devices with their start and end apart: 1 -> 0, of which waited for: 1 -> 0; matrix products, arithmetic and copies ran while one was open for 0% -> 0% of each run, Pallas kernels for 0% -> 0%
where the time goes in v1:
time: 27.4 us; the launch traced here: 27.3 us
  Pallas kernels  23.4 us (85%)
  local copies, waits for them, and re-layouts  3.25 us (12%)
  between operations  0.65 us (2%)
    pallas_call x1, Pallas kernels, per_device(): pl.pallas_call(functools.partial(kernel, (n_ta, n_sa, zs, ys, cores)), ou...  23.4 us
    unnamed x3, local copies, waits for them, and re-layouts  2.74 us

profile of v1, /device:TPU:0, one launch (start us, length us, event | category | flops | bytes accessed | tf_op | source)
XLA Modules:
  0.0 27.3 jit_solution(8866190041695333150)
XLA Ops:
  0.6 0.0 copy-start
  0.6 2.1 %copy-done = bf16[6,2,3,432,128]{4,3,2,1,0:T(8,128)(2,1)S(1)} copy-done((bf16[6,2,3,432,128]{4,3,2,1,0:T(8,128)(2,1)S(1)}, bf16[6,2,3,432,128]{4,3,2,1,0:T(8,128)(2,1)}, u32[]{:S(2)}) %copy-start) | copy-done | bytes 3981336
  2.8 23.4 %shard_map.41 = (f32[6,2,8,128]{3,2,1,0:T(8,128)S(1)}, f32[1,128]{1,0:T(1,128)S(1)}) custom-call(bf16[6,2,3,432,128]{4,3,2,1,0:T(8,128)(2,1)S(1)} %copy-done, bf16[6,2,3,432,128]{4,3,2,1,0:T(8,128)(2,1)} %sol_hbm.1), custom_call_target="tpu_custom_call" | custom-call | tf_op jit(solution)/shard_map/pallas_call | solution.py:187
  26.1 0.5 %slice_bitcast_fusion = f32[12]{0:T(128)} fusion(f32[1,128]{1,0:T(1,128)S(1)} %get-tuple-element.5), kind=kLoop, calls=%fused_computation | loop fusion | bytes 96 | tf_op jit(solution)/shard_map/squeeze | solution.py:212
  26.6 0.6 %copy.5 = f32[6,2,8,128]{3,2,1,0:T(8,128)} copy(f32[6,2,8,128]{3,2,1,0:T(8,128)S(1)} %get-tuple-element.8) | data formatting | bytes 98304
Async XLA Ops:
  0.6 2.1 %copy-start = (bf16[6,2,3,432,128]{4,3,2,1,0:T(8,128)(2,1)S(1)}, bf16[6,2,3,432,128]{4,3,2,1,0:T(8,128)(2,1)}, u32[]{:S(2)}) copy-start(bf16[6,2,3,432,128]{4,3,2,1,0:T(8,128)(2,1)} %vec_hbm.1) | copy-start | bytes 11943940

commit v2 on v1

--- a/solution.py
+++ b/solution.py
@@ -19,9 +19,20 @@
     return rest // ys, ys, cores
 
 
+def z_first(t):
+    return t % 2 == 1 and t < 4
+
+
+def put_outputs(tau_in, corr_in, tau_out, corr_out, sem):
+    copy = pltpu.make_async_copy(tau_in, tau_out, sem)
+    copy.start()
+    corr_out[...] = corr_in[0, :corr_out.shape[0]]
+    copy.wait()
+
+
 def kernel(dims, vec_hbm, sol_hbm, tau_ref, corr_ref,
-           vec, sol, part, got_core, half, got_y, quarter, got_z, norms,
-           load_sem, core_send, core_recv, y_send, y_recv, z_send, z_recv, n_send, n_recv):
+           vec, sol, part, got_core, half, got_first, quarter, got_second, norms,
+           load_sem, core_send, core_recv, first_send, first_recv, second_send, second_recv, n_send, n_recv):
     n_ta, n_sa, zs, ys, cores = dims
     slices = vec_hbm.shape[0]
     rows = tau_ref.shape[2]
@@ -71,17 +82,27 @@
             send_sem=core_send.at[t, j - 1], recv_sem=core_recv.at[t, j - 1],
             device_id={"ta": ta, "sa": core_peer(j)}) for j in range(1, cores)]
 
-    def y_copies(t):
+    def axes_of(t):
+        y_axis, z_axis = (my_y, ys, y_peer), (my_z, zs, z_peer)
+        return (z_axis, y_axis) if z_first(t) else (y_axis, z_axis)
+
+    def device_of(t, stage, position):
+        along_z = z_first(t) == (stage == 0)
+        return {"ta": ta, "sa": at(position, my_y, core) if along_z else at(my_z, position, core)}
+
+    def first_copies(t):
+        (_, size, peer), (_, other, _) = axes_of(t)
         return [pltpu.make_async_remote_copy(
-            src_ref=half.at[t, y_peer(j)], dst_ref=got_y.at[t, j - 1],
-            send_sem=y_send.at[t, j - 1], recv_sem=y_recv.at[t, j - 1],
-            device_id={"ta": ta, "sa": at(my_z, y_peer(j), core)}) for j in range(1, ys)]
-
-    def z_copies(t):
+            src_ref=half.at[t, pl.ds(peer(j) * other, other)], dst_ref=got_first.at[t, pl.ds((j - 1) * other, other)],
+            send_sem=first_send.at[t, j - 1], recv_sem=first_recv.at[t, j - 1],
+            device_id=device_of(t, 0, peer(j))) for j in range(1, size)]
+
+    def second_copies(t):
+        _, (_, size, peer) = axes_of(t)
         return [pltpu.make_async_remote_copy(
-            src_ref=quarter.at[t, z_peer(j)], dst_ref=got_z.at[t, j - 1],
-            send_sem=z_send.at[t, j - 1], recv_sem=z_recv.at[t, j - 1],
-            device_id={"ta": ta, "sa": at(z_peer(j), my_y, core)}) for j in range(1, zs)]
+            src_ref=quarter.at[t, peer(j)], dst_ref=got_second.at[t, j - 1],
+            send_sem=second_send.at[t, j - 1], recv_sem=second_recv.at[t, j - 1],
+            device_id=device_of(t, 1, peer(j))) for j in range(1, size)]
 
     def compute(t):
         for one in loads[t]:
@@ -95,7 +116,7 @@
         for p in range(2):
             for d in range(n_sa):
                 c, y, z = d % cores, d // cores % ys, d // (cores * ys)
-                part[t, c, y, z, p] = both[p][d * rows:(d + 1) * rows]
+                part[t, c, z * ys + y if z_first(t) else y * zs + z, p] = both[p][d * rows:(d + 1) * rows]
         if t == 0:
             pl.semaphore_wait(barrier, greeted)
         for one in core_copies(t):
@@ -108,25 +129,27 @@
         for j in range(1, cores):
             total = total + got_core[t, j - 1]
         half[t] = total
-        for one in y_copies(t):
-            one.start()
-
-    def after_y(t):
-        for one in y_copies(t):
+        for one in first_copies(t):
+            one.start()
+
+    def after_first(t):
+        for one in first_copies(t):
             one.wait_recv()
-        total = half[t, my_y]
-        for j in range(1, ys):
-            total = total + got_y[t, j - 1]
-        quarter[t] = total
-        for one in z_copies(t):
-            one.start()
-
-    def after_z(t):
-        for one in z_copies(t):
+        (own, size, _), (_, other, _) = axes_of(t)
+        total = half[t, pl.ds(own * other, other)]
+        for j in range(1, size):
+            total = total + got_first[t, (j - 1) * other:j * other]
+        quarter[t, :other] = total
+        for one in second_copies(t):
+            one.start()
+
+    def after_second(t):
+        for one in second_copies(t):
             one.wait_recv()
-        total = quarter[t, my_z]
-        for j in range(1, zs):
-            total = total + got_z[t, j - 1]
+        _, (own, size, _) = axes_of(t)
+        total = quarter[t, own]
+        for j in range(1, size):
+            total = total + got_second[t, j - 1]
         tau_ref[t] = total
         square = total * total
         return jnp.sum(square[0] + square[1], axis=0, keepdims=True)
@@ -138,12 +161,12 @@
         if t >= lag:
             after_core(t - lag)
     for t in range(slices):
-        after_y(t)
+        after_first(t)
     width = norms.shape[-1]
     lane = lax.broadcasted_iota(jnp.int32, (1, width), 1)
     mine = jnp.zeros((1, width), jnp.float32)
     for t in range(slices):
-        norm = jnp.sum(after_z(t), axis=1, keepdims=True)
+        norm = jnp.sum(after_second(t), axis=1, keepdims=True)
         mine = mine + jnp.where(lane == ta * slices + t, norm, 0.0)
     place = ta * n_sa + me
     norms[place] = mine
@@ -161,7 +184,7 @@
         norm_copy(j).start()
 
     for t in range(slices):
-        for one in core_copies(t) + y_copies(t) + z_copies(t):
+        for one in core_copies(t) + first_copies(t) + second_copies(t):
             one.wait_send()
     rest = norms.at[pl.ds(0, everyone - 1)]
     whole = pltpu.make_async_remote_copy(
@@ -193,23 +216,29 @@
             scratch_shapes=[
                 pltpu.VMEM(vecs.shape, vecs.dtype),
                 pltpu.VMEM(sols.shape, sols.dtype),
-                pltpu.VMEM((slices, cores, ys, zs) + block, f32),
-                pltpu.VMEM((slices, max(cores - 1, 1), ys, zs) + block, f32),
-                pltpu.VMEM((slices, ys, zs) + block, f32),
-                pltpu.VMEM((slices, max(ys - 1, 1), zs) + block, f32),
-                pltpu.VMEM((slices, zs) + block, f32),
-                pltpu.VMEM((slices, max(zs - 1, 1)) + block, f32),
+                pltpu.VMEM((slices, cores, ys * zs) + block, f32),
+                pltpu.VMEM((slices, max(cores - 1, 1), ys * zs) + block, f32),
+                pltpu.VMEM((slices, ys * zs) + block, f32),
+                pltpu.VMEM((slices, ys * zs) + block, f32),
+                pltpu.VMEM((slices, max(ys, zs)) + block, f32),
+                pltpu.VMEM((slices, max(ys, zs)) + block, f32),
                 pltpu.VMEM((n_ta * n_sa, 1, width), f32),
                 dma((slices, 2)),
                 dma((slices, max(cores - 1, 1))), dma((slices, max(cores - 1, 1))),
-                dma((slices, max(ys - 1, 1))), dma((slices, max(ys - 1, 1))),
-                dma((slices, max(zs - 1, 1))), dma((slices, max(zs - 1, 1))),
+                dma((slices, max(ys, zs))), dma((slices, max(ys, zs))),
+                dma((slices, max(ys, zs))), dma((slices, max(ys, zs))),
                 dma, dma,
             ],
             compiler_params=pltpu.CompilerParams(
-                collective_id=0, has_side_effects=True, vmem_limit_bytes=48 * 1024 * 1024),
+                collective_id=0, has_side_effects=True, vmem_limit_bytes=64_000_000),
         )(vecs, sols)
-        return tau, corr[0, :n_ta * slices]
+        return pl.pallas_call(
+            put_outputs,
+            out_shape=(jax.ShapeDtypeStruct(tau.shape, f32), jax.ShapeDtypeStruct((n_ta * slices,), f32)),
+            in_specs=[pl.BlockSpec(memory_space=pltpu.VMEM)] * 2,
+            out_specs=[pl.BlockSpec(memory_space=pltpu.HBM), pl.BlockSpec(memory_space=pltpu.VMEM)],
+            scratch_shapes=[dma],
+        )(tau, corr)
 
     in_specs = (P("ta", None, None, "sa", None), P("ta", None, None, "sa", None))
     out_specs = (P("ta", None, "sa", None), P())

time: 27.4 us -> 25.5 us (0.931)
  local copies, waits for them, and re-layouts: 3.25 us -> 0 us
  Pallas kernels: 23.4 us -> 24.7 us
    unnamed x3 -> x0, local copies, waits for them, and re-layouts: 2.74 us -> none
    pallas_call x0 -> x1, Pallas kernels: none -> 1.94 us  [per_device(): pl.pallas_call(put_outputs, out_shape=(jax.ShapeDtypeStruct(tau.shape, f3...]
    pallas_call x1, Pallas kernels: 23.4 us -> 22.8 us  [per_device(): pl.pallas_call(functools.partial(kernel, (n_ta, n_sa, zs, ys, cores)), ou...]
    squeeze x1 -> x0, local copies, waits for them, and re-layouts: 0.51 us -> none  [per_device(): return (tau, corr[0, :n_ta * slices])]
where the time goes in v2:
time: 25.5 us; the launch traced here: 25.4 us
  Pallas kernels  24.7 us (97%)
  between operations  0.64 us (3%)
    pallas_call x1, Pallas kernels, per_device(): pl.pallas_call(functools.partial(kernel, (n_ta, n_sa, zs, ys, cores)), ou...  22.8 us
    pallas_call x1, Pallas kernels, per_device(): pl.pallas_call(put_outputs, out_shape=(jax.ShapeDtypeStruct(tau.shape, f3...  1.94 us

profile of v2, /device:TPU:0, one launch (start us, length us, event | category | flops | bytes accessed | tf_op | source)
XLA Modules:
  0.0 25.4 jit_solution(9121637778715023732)
XLA Ops:
  0.6 22.8 %shard_map.41 = (f32[6,2,8,128]{3,2,1,0:T(8,128)}, f32[1,128]{1,0:T(1,128)}) custom-call(bf16[6,2,3,432,128]{4,3,2,1,0:T(8,128)(2,1)} %vec_hbm.1, bf16[6,2,3,432,128]{4,3,2,1,0:T(8,128)(2,1)} %sol_hbm.1), custom_call_target="tpu_custom_call" | custom-call | tf_op jit(solution)/shard_map/pallas_call | solution.py:210
  23.4 1.9 %shard_map.42 = (f32[6,2,8,128]{3,2,1,0:T(8,128)}, f32[12]{0:T(128)}) custom-call(f32[6,2,8,128]{3,2,1,0:T(8,128)} %get-tuple-element.4.tau_in, f32[1,128]{1,0:T(1,128)} %get-tuple-element.5.corr_in), custom_call_target="tpu_custom_call" | custom-call | tf_op jit(solution)/shard_map/pallas_call | solution.py:235
